TPU v7x, 32 devices: a whole 2x2x4 slice. The times are simulated.
32 devices in a mesh: gx: 8 (over z, x), gy: 4 (over y, core).
Axes of the slice: x: 2, y: 2, z: 4, core: 2. Of those that a mesh axis runs over, the one named last changes fastest.
Arguments:
- species: float32 [53, 32, 32, 128], P(None, 'gx', 'gy'), may hold values from -6 to 6
- diffusion: float32 [53], replicated, may hold values from 0.02 to 0.15
- class_rate: float32 [4], replicated, may hold values from 0.2 to 1
- mixing: float32 [53, 53], replicated, may hold values from -0.3 to 0.3
- inverses: float32 [4, 53, 53], replicated, may hold values from -0.01 to 0.12
- newton_counts: int32 [4], replicated, may hold values from 1 to 8, as said below
- cell_class: int32 [32, 32, 128], P('gx', 'gy'), may hold values from 0 to 3
Outputs:
- updated: float32 [53, 32, 32, 128], P(None, 'gx', 'gy')
Inputs may be any that keep to these rules, and one draw needn't show every extreme that they name: `newton_counts`: nondecreasing in the class; the last class takes 8.
All inputs are finite; a program needn't handle non-finite values.
Results may differ from a plain program's by a relative error of at most 0.0003.
Values sent between devices are 32-bit elements; how exact they have to be, the bound alone decides.
A program may use at most 64 MiB of HBM per device.

v0:
```python
import math

import jax
import jax.numpy as jnp
from jax import lax
from jax.sharding import PartitionSpec as P

SPEC = 53
NCLASS = 4


def extended(block, sides, width):
    for axis, dim in sides:
        count = lax.axis_size(axis)
        forward = [(i, i + 1) for i in range(count - 1)]
        backward = [(target, source) for source, target in forward]
        low = lax.ppermute(
            lax.slice_in_dim(block, block.shape[dim] - width, None, axis=dim), axis, forward
        )
        high = lax.ppermute(lax.slice_in_dim(block, 0, width, axis=dim), axis, backward)
        block = jnp.concatenate([low, block, high], axis=dim)
    return block


def laplace(grid_field):
    padded = extended(grid_field, (("gx", 1), ("gy", 2)), 1)
    padded_z = jnp.pad(padded, ((0, 0), (0, 0), (0, 0), (1, 1)))
    total = padded_z[:, 2:, 1:-1, 1:-1] + padded_z[:, :-2, 1:-1, 1:-1]
    total = total + padded_z[:, 1:-1, 2:, 1:-1] + padded_z[:, 1:-1, :-2, 1:-1]
    total = total + padded_z[:, 1:-1, 1:-1, 2:] + padded_z[:, 1:-1, 1:-1, :-2]
    return total - 6.0 * grid_field


def newton_block(target, classes, class_rate, mixing, inverses, newton_counts):
    class_mask = classes[None, :] == jnp.arange(NCLASS, dtype=jnp.int32)[:, None]
    weights = class_mask.astype(jnp.float32)
    cell_rate = jnp.sum(class_rate[:, None] * weights, axis=0)
    cell_count = jnp.sum(jnp.where(class_mask, newton_counts[:, None], 0), axis=0)
    block_limit = jnp.max(cell_count)
    lowest = jnp.min(classes)
    highest = jnp.max(classes)
    single_inverse = lax.dynamic_index_in_dim(inverses, lowest, 0, keepdims=False)

    def one_class(residual):
        return jnp.dot(single_inverse, residual, precision=lax.Precision.HIGHEST)

    def mixed_classes(residual):
        correction = jnp.zeros_like(residual)
        for which in range(NCLASS):
            correction = correction + weights[which] * jnp.dot(
                inverses[which], residual, precision=lax.Precision.HIGHEST
            )
        return correction

    def newton_step(k, state):
        source = jnp.dot(mixing, jnp.tanh(state), precision=lax.Precision.HIGHEST) - state
        residual = state - target - cell_rate * source
        correction = lax.cond(lowest == highest, one_class, mixed_classes, residual)
        return jnp.where(k < cell_count, state - correction, state)

    return lax.fori_loop(0, block_limit, newton_step, target)


def solve_cells(flat_cells, classes, class_rate, mixing, inverses, newton_counts):
    total_cells = flat_cells.shape[1]
    block_size = math.gcd(total_cells, 512)
    blocks = total_cells // block_size
    sorted_order = jnp.argsort(classes, stable=True)
    inverse_order = jnp.argsort(sorted_order, stable=True)
    sorted_cells = jnp.take(flat_cells, sorted_order, axis=1)
    sorted_class = jnp.take(classes, sorted_order, axis=0)
    cell_blocks = jnp.moveaxis(sorted_cells.reshape(SPEC, blocks, block_size), 1, 0)
    class_blocks = sorted_class.reshape(blocks, block_size)

    def solve_one(pair):
        return newton_block(pair[0], pair[1], class_rate, mixing, inverses, newton_counts)

    solved = lax.map(solve_one, (cell_blocks, class_blocks))
    solved = jnp.moveaxis(solved, 0, 1).reshape(SPEC, total_cells)
    return jnp.take(solved, inverse_order, axis=1)


def local(species, diffusion, class_rate, mixing, inverses, newton_counts, cell_class):
    scaled = diffusion[:, None, None, None]
    forcing = laplace(species) * scaled
    target = species + forcing
    flat_cells = target.reshape(SPEC, -1)
    classes = cell_class.reshape(-1)
    section_flat = solve_cells(flat_cells, classes, class_rate, mixing, inverses, newton_counts)
    section_value = section_flat.reshape(species.shape)
    second = laplace(section_value) * scaled
    return section_value + 0.5 * (second - forcing)


def solution(mesh):
    in_specs = (P(None, "gx", "gy", None), P(), P(), P(), P(), P(), P("gx", "gy", None))
    out_specs = P(None, "gx", "gy", None)
    return jax.shard_map(local, mesh=mesh, in_specs=in_specs, out_specs=out_specs, check_vma=False)
```

profile of v0, /device:TPU:20, one launch (start us, length us, event | category | flops | bytes accessed | tf_op | source)
XLA Modules:
  0.0 227.4 jit_solution(748454282101404453)
XLA Ops:
  0.0 1.7 copy.55
  1.7 3.4 %collective-permute-start.1 = (f32[53,1,8,128]{3,0,2,1:T(8,128)S(1)}, f32[53,1,8,128]{3,0,2,1:T(8,128)S(1)}, u32[]{:S(2)}, u32[]{:S(2)}) collective-permute-start(f32[53,1,8,128]{3,0,2,1:T(8,128)S(1)} %get-tuple-element.325), channel_id=1, source_target_pairs={{0,4},{4,8},{8,12},{12,16},{16,20},{20,24},{24,28},{1,5},{5,9},{9,... | collective-permute-start | bytes 651272 | tf_op jit(solution)/shard_map/ppermute | solution.py:17
  5.1 3.3 %collective-permute-start = (f32[53,1,8,128]{3,0,2,1:T(8,128)S(1)}, f32[53,1,8,128]{3,0,2,1:T(8,128)S(1)}, u32[]{:S(2)}, u32[]{:S(2)}) collective-permute-start(f32[53,1,8,128]{3,0,2,1:T(8,128)S(1)} %get-tuple-element.324), channel_id=1, source_target_pairs={{4,0},{8,4},{12,8},{16,12},{20,16},{24,20},{28,24},{5,1},{9,5},{13... | collective-permute-start | bytes 651272 | tf_op jit(solution)/shard_map/ppermute | solution.py:20
  8.5 6.5 %sort.31 = (s32[4096]{0:T(1024)}, s32[4096]{0:T(1024)S(1)}) sort(s32[4096]{0:T(1024)} %bitcast.51, s32[4096]{0:T(1024)S(1)} %iota.11), dimensions={0}, to_apply=%region_0.1 | sort | flops 49152 | bytes 65536 | tf_op jit(solution)/shard_map/jit(argsort)/sort | solution.py:68
  15.0 23.0 %gather_fusion = s32[4096]{0:T(1024)S(1)} fusion(s32[4096]{0:T(1024)S(1)} %bitcast.52, s32[4096]{0:T(1024)S(1)} %fusion.31), kind=kCustom, calls=%fused_computation.2 | custom fusion | bytes 49152 | tf_op jit(solution)/shard_map/jit(_take)/gather | solution.py:71
  38.1 5.8 %sort.32 = (s32[4096]{0:T(1024)}, s32[4096]{0:T(1024)S(1)}) sort(s32[4096]{0:T(1024)S(1)} %get-tuple-element.208, s32[4096]{0:T(1024)S(1)} %iota.12), dimensions={0}, to_apply=%region_12.14 | sort | flops 49152 | bytes 65536 | tf_op jit(solution)/shard_map/jit(argsort)/sort | solution.py:69
  44.6 1.9 collective-permute-start.2
  46.5 2.4 %collective-permute-start.3 = (f32[53,6,1,128]{3,0,2,1:T(8,128)S(1)}, f32[53,6,1,128]{3,0,2,1:T(8,128)S(1)}, u32[]{:S(2)}, u32[]{:S(2)}) collective-permute-start(f32[53,6,1,128]{3,0,2,1:T(8,128)S(1)} %get-tuple-element.320), channel_id=1, source_target_pairs={{0,1},{1,2},{2,3},{4,5},{5,6},{6,7},{8,9},{9,10},{10,11},{12,13},{... | collective-permute-start | bytes 488456 | tf_op jit(solution)/shard_map/ppermute | solution.py:17
  49.4 3.8 %collective-permute-done.3 = f32[53,6,1,128]{3,0,2,1:T(8,128)S(1)} collective-permute-done((f32[53,6,1,128]{3,0,2,1:T(8,128)S(1)}, f32[53,6,1,128]{3,0,2,1:T(8,128)S(1)}, u32[]{:S(2)}, u32[]{:S(2)}) %collective-permute-start.3) | collective-permute-done | bytes 162848 | tf_op jit(solution)/shard_map/ppermute | solution.py:17
  54.2 1.8 copy_add_fusion
  56.6 14.1 %gather_fusion.1 = f32[4096,53]{1,0:T(8,128)} fusion(f32[53,4096]{0,1:T(8,128)S(1)} %bitcast.53, s32[4096]{0:T(1024)S(1)} %fusion.31), kind=kCustom, calls=%fused_computation.clone | custom fusion | bytes 1753088 | tf_op jit(solution)/shard_map/jit(_take)/gather | solution.py:70
  70.7 3.6 %broadcast_select_fusion.1 = f32[4096,53]{1,0:T(8,128)S(1)} fusion(f32[4096,53]{1,0:T(8,128)} %gather_fusion.1, pred[4096]{0:T(1024)(128)(4,1)S(1)} %get-tuple-element.311), kind=kLoop, calls=%fused_computation.44 | loop fusion | flops 217088 | bytes 1740800 | tf_op jit(solution)/shard_map/jit(_take)/select_n | solution.py:70
  75.1 93.6 %while.24 = (s32[]{:T(128)}, f32[8,53,512]{2,1,0:T(8,128)}, f32[8,53,512]{2,1,0:T(8,128)S(1)}, s32[8,512]{1,0:T(8,128)S(1)}, s32[4]{0:T(128)S(1)}, /*index=5*/f3...) while((s32[]{:T(128)}, f32[8,53,512]{2,1,0:T(8,128)}, ...), condition=%wide.region_11.13_spmd, body=%wide.region_1.12_spmd.sunk | while | flops 86662656 | bytes 2749358 | solution.py:78
  79.7 1.7 while.25
  86.7 1.7 while.25
  93.7 1.7 while.25
  100.8 1.7 while.25
  107.8 1.7 while.25
  114.8 12.3 %while.25 = (s32[]{:T(128)}, f32[53,512]{1,0:T(8,128)S(1)}, s32[]{:T(128)}, s32[512]{0:T(512)S(1)}, pred[]{:T(512)}, /*index=5*/f32[53,512]{1,0:T(8,128)S(1)}, f...) while((s32[]{:T(128)}, f32[53,512]{1,0:T(8,128)S(1)}, ...), condition=%wide.region_10.11_spmd.clone, body=%wide.region_7.10_spmd.clone.sunk | while | flops 86649856 | bytes 2054290 | solution.py:61
  115.7 1.0 conditional.3
  117.6 1.0 conditional.3
  119.6 1.0 conditional.3
  121.5 1.0 conditional.3
  123.5 1.0 conditional.3
  125.4 1.0 conditional.3
  132.4 14.2 %while.25 = (s32[]{:T(128)}, f32[53,512]{1,0:T(8,128)S(1)}, s32[]{:T(128)}, s32[512]{0:T(512)S(1)}, pred[]{:T(512)}, /*index=5*/f32[53,512]{1,0:T(8,128)S(1)}, f...) while((s32[]{:T(128)}, f32[53,512]{1,0:T(8,128)S(1)}, ...), condition=%wide.region_10.11_spmd.clone, body=%wide.region_7.10_spmd.clone.sunk | while | flops 86649856 | bytes 2054290 | solution.py:61
  133.2 1.0 conditional.3
  135.2 1.0 conditional.3
  141.0 1.0 conditional.3
  143.0 1.0 conditional.3
  144.9 1.0 conditional.3
  151.9 16.2 %while.25 = (s32[]{:T(128)}, f32[53,512]{1,0:T(8,128)S(1)}, s32[]{:T(128)}, s32[512]{0:T(512)S(1)}, pred[]{:T(512)}, /*index=5*/f32[53,512]{1,0:T(8,128)S(1)}, f...) while((s32[]{:T(128)}, f32[53,512]{1,0:T(8,128)S(1)}, ...), condition=%wide.region_10.11_spmd.clone, body=%wide.region_7.10_spmd.clone.sunk | while | flops 86649856 | bytes 2054290 | solution.py:61
  152.7 1.0 conditional.3
  154.7 1.0 conditional.3
  156.6 1.0 conditional.3
  160.5 1.0 conditional.3
  168.7 1.8 copy.59
  170.5 14.1 %gather_fusion.2 = f32[4096,53]{1,0:T(8,128)} fusion(f32[53,4096]{0,1:T(8,128)S(1)} %bitcast.54, s32[4096]{0:T(1024)S(1)} %fusion.32), kind=kCustom, calls=%fused_computation.1.clone | custom fusion | bytes 1753088 | tf_op jit(solution)/shard_map/jit(_take)/gather | solution.py:80
  184.6 3.6 %broadcast_select_fusion = f32[4096,53]{1,0:T(8,128)S(1)} fusion(f32[4096,53]{1,0:T(8,128)} %gather_fusion.2, pred[4096]{0:T(1024)(128)(4,1)S(1)} %compare_and_fusion), kind=kLoop, calls=%fused_computation.43 | loop fusion | flops 217088 | bytes 1740800 | tf_op jit(solution)/shard_map/jit(_take)/select_n | solution.py:80
  188.9 1.9 collective-permute-start.4
  190.9 16.8 %collective-permute-start.5 = (f32[53,1,8,128]{3,0,2,1:T(8,128)S(1)}, f32[53,1,8,128]{3,0,2,1:T(8,128)S(1)}, u32[]{:S(2)}, u32[]{:S(2)}) collective-permute-start(f32[53,1,8,128]{3,0,2,1:T(8,128)S(1)} %get-tuple-element.322), channel_id=1, source_target_pairs={{0,4},{4,8},{8,12},{12,16},{16,20},{20,24},{24,28},{1,5},{5,9},{9,... | collective-permute-start | bytes 651272 | tf_op jit(solution)/shard_map/ppermute | solution.py:17
  207.7 1.9 collective-permute-done.4
  209.6 3.9 %collective-permute-done.5 = f32[53,1,8,128]{3,0,2,1:T(8,128)S(1)} collective-permute-done((f32[53,1,8,128]{3,0,2,1:T(8,128)S(1)}, f32[53,1,8,128]{3,0,2,1:T(8,128)S(1)}, u32[]{:S(2)}, u32[]{:S(2)}) %collective-permute-start.5) | collective-permute-done | bytes 217120 | tf_op jit(solution)/shard_map/ppermute | solution.py:17
  213.6 2.8 %collective-permute-start.6 = (f32[53,6,1,128]{3,0,2,1:T(8,128)S(1)}, f32[53,6,1,128]{3,0,2,1:T(8,128)S(1)}, u32[]{:S(2)}, u32[]{:S(2)}) collective-permute-start(f32[53,6,1,128]{3,0,2,1:T(8,128)S(1)} %get-tuple-element.319), channel_id=1, source_target_pairs={{1,0},{2,1},{3,2},{5,4},{6,5},{7,6},{9,8},{10,9},{11,10},{13,12},{... | collective-permute-start | bytes 488456 | tf_op jit(solution)/shard_map/ppermute | solution.py:20
  216.4 1.9 collective-permute-start.7
  219.3 3.8 %collective-permute-done.7 = f32[53,6,1,128]{3,0,2,1:T(8,128)S(1)} collective-permute-done((f32[53,6,1,128]{3,0,2,1:T(8,128)S(1)}, f32[53,6,1,128]{3,0,2,1:T(8,128)S(1)}, u32[]{:S(2)}, u32[]{:S(2)}) %collective-permute-start.7) | collective-permute-done | bytes 162848 | tf_op jit(solution)/shard_map/ppermute | solution.py:17
  223.1 2.7 %select_maximum_fusion = f32[53,6,10,130]{3,0,2,1:T(8,128)S(1)} fusion(f32[53,6,1,128]{3,0,2,1:T(8,128)S(1)} %collective-permute-done.6, f32[53,6,1,128]{3,0,2,1:T(8,128)S(1)} %collective-permute-done.7, f32[53,1,8,128]{3,0,2,1:T(8,128)S(1)} %collective-permute-done.4, f32[53,4,8,128]{3,0,2,1:T(8,128)S(1)} %copy.66, ...), kind=kLoop, calls=%fused_computation.36 | loop fusion | flops 4960800 | bytes 3281760 | tf_op jit(solution)/shard_map/concatenate | solution.py:21
  226.3 1.1 copy.67
  (330 shorter events, 60.2 us)
Async XLA Ops:
  0.0 15.0 %copy-start = (s32[4,8,128]{2,1,0:T(8,128)S(1)}, s32[4,8,128]{2,1,0:T(8,128)}, u32[]{:S(2)}) copy-start(s32[4,8,128]{2,1,0:T(8,128)} %param.21) | copy-start | bytes 49156
  1.7 42.2 %collective-permute-start.1 = (f32[53,1,8,128]{3,0,2,1:T(8,128)S(1)}, f32[53,1,8,128]{3,0,2,1:T(8,128)S(1)}, u32[]{:S(2)}, u32[]{:S(2)}) collective-permute-start(f32[53,1,8,128]{3,0,2,1:T(8,128)S(1)} %get-tuple-element.325), channel_id=1, source_target_pairs={{0,4},{4,8},{8,12},{12,16},{16,20},{20,24},{24,28},{1,5},{5,9},{9,... | collective-permute-start | bytes 651272 | tf_op jit(solution)/shard_map/ppermute | solution.py:17
  5.1 39.4 %collective-permute-start = (f32[53,1,8,128]{3,0,2,1:T(8,128)S(1)}, f32[53,1,8,128]{3,0,2,1:T(8,128)S(1)}, u32[]{:S(2)}, u32[]{:S(2)}) collective-permute-start(f32[53,1,8,128]{3,0,2,1:T(8,128)S(1)} %get-tuple-element.324), channel_id=1, source_target_pairs={{4,0},{8,4},{12,8},{16,12},{20,16},{24,20},{28,24},{5,1},{9,5},{13... | collective-permute-start | bytes 651272 | tf_op jit(solution)/shard_map/ppermute | solution.py:20
  15.0 23.1 %copy-start.4 = (f32[4,53,53]{2,0,1:T(4,128)S(1)}, f32[4,53,53]{2,0,1:T(4,128)}, u32[]{:S(2)}) copy-start(f32[4,53,53]{2,0,1:T(4,128)} %param.19) | copy-start | bytes 134836
  15.0 28.9 %copy-start.2 = (f32[53,4,8,128]{3,2,1,0:T(8,128)S(1)}, f32[53,4,8,128]{3,2,1,0:T(8,128)}, u32[]{:S(2)}) copy-start(f32[53,4,8,128]{3,2,1,0:T(8,128)} %param.15) | copy-start | bytes 2605060
  44.5 9.7 %copy-start.7 = (f32[53]{0:T(128)S(1)}, f32[53]{0:T(128)}, u32[]{:S(2)}) copy-start(f32[53]{0:T(128)} %param.16) | copy-start | bytes 640
  44.6 4.8 %collective-permute-start.2 = (f32[53,6,1,128]{3,0,2,1:T(8,128)S(1)}, f32[53,6,1,128]{3,0,2,1:T(8,128)S(1)}, u32[]{:S(2)}, u32[]{:S(2)}) collective-permute-start(f32[53,6,1,128]{3,0,2,1:T(8,128)S(1)} %get-tuple-element.321), channel_id=1, source_target_pairs={{1,0},{2,1},{3,2},{5,4},{6,5},{7,6},{9,8},{10,9},{11,10},{13,12},{... | collective-permute-start | bytes 488456 | tf_op jit(solution)/shard_map/ppermute | solution.py:20
  46.5 6.7 %collective-permute-start.3 = (f32[53,6,1,128]{3,0,2,1:T(8,128)S(1)}, f32[53,6,1,128]{3,0,2,1:T(8,128)S(1)}, u32[]{:S(2)}, u32[]{:S(2)}) collective-permute-start(f32[53,6,1,128]{3,0,2,1:T(8,128)S(1)} %get-tuple-element.320), channel_id=1, source_target_pairs={{0,1},{1,2},{2,3},{4,5},{5,6},{6,7},{8,9},{9,10},{10,11},{12,13},{... | collective-permute-start | bytes 488456 | tf_op jit(solution)/shard_map/ppermute | solution.py:17
  70.7 4.3 %copy-start.1 = (f32[53,53]{1,0:T(8,128)S(1)}, f32[53,53]{1,0:T(8,128)}, u32[]{:S(2)}) copy-start(f32[53,53]{1,0:T(8,128)} %param.18) | copy-start | bytes 33712
  70.7 4.3 %copy-start.5 = (s32[4]{0:T(128)S(1)}, s32[4]{0:T(128)}, u32[]{:S(2)}) copy-start(s32[4]{0:T(128)} %param.20) | copy-start | bytes 52
  70.7 4.3 %copy-start.6 = (f32[4]{0:T(128)S(1)}, f32[4]{0:T(128)}, u32[]{:S(2)}) copy-start(f32[4]{0:T(128)} %param.17) | copy-start | bytes 52
  188.9 20.7 %collective-permute-start.4 = (f32[53,1,8,128]{3,0,2,1:T(8,128)S(1)}, f32[53,1,8,128]{3,0,2,1:T(8,128)S(1)}, u32[]{:S(2)}, u32[]{:S(2)}) collective-permute-start(f32[53,1,8,128]{3,0,2,1:T(8,128)S(1)} %get-tuple-element.323), channel_id=1, source_target_pairs={{4,0},{8,4},{12,8},{16,12},{20,16},{24,20},{28,24},{5,1},{9,5},{13... | collective-permute-start | bytes 651272 | tf_op jit(solution)/shard_map/ppermute | solution.py:20
  190.9 34.9 %copy-start.3 = (f32[53,4,8,128]{3,0,2,1:T(8,128)S(1)}, f32[53,4,8,128]{3,0,2,1:T(8,128)}, u32[]{:S(2)}) copy-start(f32[53,4,8,128]{3,0,2,1:T(8,128)} %get-tuple-element.313) | copy-start | bytes 2605060
  190.9 22.7 %collective-permute-start.5 = (f32[53,1,8,128]{3,0,2,1:T(8,128)S(1)}, f32[53,1,8,128]{3,0,2,1:T(8,128)S(1)}, u32[]{:S(2)}, u32[]{:S(2)}) collective-permute-start(f32[53,1,8,128]{3,0,2,1:T(8,128)S(1)} %get-tuple-element.322), channel_id=1, source_target_pairs={{0,4},{4,8},{8,12},{12,16},{16,20},{20,24},{24,28},{1,5},{5,9},{9,... | collective-permute-start | bytes 651272 | tf_op jit(solution)/shard_map/ppermute | solution.py:17
  213.6 5.7 %collective-permute-start.6 = (f32[53,6,1,128]{3,0,2,1:T(8,128)S(1)}, f32[53,6,1,128]{3,0,2,1:T(8,128)S(1)}, u32[]{:S(2)}, u32[]{:S(2)}) collective-permute-start(f32[53,6,1,128]{3,0,2,1:T(8,128)S(1)} %get-tuple-element.319), channel_id=1, source_target_pairs={{1,0},{2,1},{3,2},{5,4},{6,5},{7,6},{9,8},{10,9},{11,10},{13,12},{... | collective-permute-start | bytes 488456 | tf_op jit(solution)/shard_map/ppermute | solution.py:20
  216.4 6.7 %collective-permute-start.7 = (f32[53,6,1,128]{3,0,2,1:T(8,128)S(1)}, f32[53,6,1,128]{3,0,2,1:T(8,128)S(1)}, u32[]{:S(2)}, u32[]{:S(2)}) collective-permute-start(f32[53,6,1,128]{3,0,2,1:T(8,128)S(1)} %get-tuple-element.318), channel_id=1, source_target_pairs={{0,1},{1,2},{2,3},{4,5},{5,6},{6,7},{8,9},{9,10},{10,11},{12,13},{... | collective-permute-start | bytes 488456 | tf_op jit(solution)/shard_map/ppermute | solution.py:17
where the time goes:
time: 225 us; the launch traced here: 227 us
  local copies, waits for them, and re-layouts  64.1 us (28%)
  loops' own time  46.5 us (21%)
  other arithmetic  38.7 us (17%)
  starting transfers between devices  34.6 us (15%)
  matrix products  28.3 us (13%)
  waiting for transfers between devices  14.9 us (7%)
    another operation x1, loops' own time, solve_cells(): solved = lax.map(solve_one, (cell_blocks, class_blocks))  25.1 us
    ppermute x4, starting transfers between devices, extended(): lax.ppermute(lax.slice_in_dim(block, block.shape[dim] - width, None, axis...  24.6 us
    gather x1, local copies, waits for them, and re-layouts, solve_cells(): sorted_class = jnp.take(classes, sorted_order, axis=0)  23 us
    dot_general x84, matrix products, mixed_classes(): jnp.dot(inverses[which], residual, precision=lax.Precision.HIGHEST)  20.5 us
    another operation x8, loops' own time, newton_block(): return lax.fori_loop(0, block_limit, newton_step, target)  20.3 us
    gather x1, local copies, waits for them, and re-layouts, solve_cells(): sorted_cells = jnp.take(flat_cells, sorted_order, axis=1)  14.1 us
    gather x1, local copies, waits for them, and re-layouts, solve_cells(): return jnp.take(solved, inverse_order, axis=1)  14.1 us
    ppermute x4, waiting for transfers between devices, extended(): lax.ppermute(lax.slice_in_dim(block, block.shape[dim] - width, None, axis...  11.5 us
  transfers between devices with their start and end apart: 8, of which 6 were waited for; matrix products, arithmetic and copies ran while one was open for 16% of the time, Pallas kernels for 0%

commit v1 on v0

v1 whole, which is shorter than its diff:
```python
import functools

import jax
import jax.numpy as jnp
from jax import lax
from jax.experimental import pallas as pl
from jax.experimental.pallas import tpu as pltpu
from jax.sharding import PartitionSpec as P

NMAX = 8
CHUNK = 2
MESH = pl.DeviceIdType.MESH
F32 = jnp.float32
BF16 = jnp.bfloat16


def kernel(
    dims,
    species_hbm, diffusion_ref, rate_ref, mixing_ref, inverses_ref, counts_ref, class_ref,
    out_ref,
    raw, ext, ext2, forcing, target, coef, square, mix_w, inv_w,
    load_sem, xs_send, xs_recv, ys_send, ys_recv,
):
    spec, nx, ny, nz, nclass = dims
    rows = nx * ny
    pad = ext.shape[2]
    chunks = ny // CHUNK
    gx, gy = lax.axis_index("gx"), lax.axis_index("gy")
    sx, sy = lax.axis_size("gx"), lax.axis_size("gy")
    has_x = (gx > 0, gx < sx - 1)
    has_y = (gy > 0, gy < sy - 1)
    to_x = ((gx - 1, gy), (gx + 1, gy))
    to_y = ((gx, gy - 1), (gx, gy + 1))

    load = pltpu.make_async_copy(species_hbm, raw, load_sem)
    load.start()

    barrier = pltpu.get_barrier_semaphore()
    for has, to in zip(has_x + has_y, to_x + to_y):
        @pl.when(has)
        def _():
            pl.semaphore_signal(barrier, inc=1, device_id=to, device_id_type=MESH)

    def x_copy(stage, side, c):
        buf = (ext, ext2)[stage]
        src_row, dst_row = (1, nx + 1) if side == 0 else (nx, 0)
        ys = pl.ds(1 + c * CHUNK, CHUNK)
        return pltpu.make_async_remote_copy(
            src_ref=buf.at[src_row, ys], dst_ref=buf.at[dst_row, ys],
            send_sem=xs_send.at[stage, side, c], recv_sem=xs_recv.at[stage, side, c],
            device_id=to_x[side], device_id_type=MESH)

    def y_copy(stage, side):
        buf = (ext, ext2)[stage]
        src_col, dst_col = (1, ny + 1) if side == 0 else (ny, 0)
        return pltpu.make_async_remote_copy(
            src_ref=buf.at[pl.ds(1, nx), src_col], dst_ref=buf.at[pl.ds(1, nx), dst_col],
            send_sem=ys_send.at[stage, side], recv_sem=ys_recv.at[stage, side],
            device_id=to_y[side], device_id_type=MESH)

    def x_arrive(stage, c):
        for side in (0, 1):
            @pl.when(has_x[side])
            def _():
                x_copy(stage, 1 - side, c).wait_recv()

    def y_arrive(stage):
        for side in (0, 1):
            @pl.when(has_y[side])
            def _():
                y_copy(stage, 1 - side).wait_recv()

    zero_col = jnp.zeros((pad, nz), F32)
    for side in (0, 1):
        @pl.when(jnp.logical_not(has_x[side]))
        def _():
            for buf in (ext, ext2):
                for y in range(ny):
                    buf[(0, nx + 1)[side], y + 1] = zero_col
        @pl.when(jnp.logical_not(has_y[side]))
        def _():
            for buf in (ext, ext2):
                for x in range(nx):
                    buf[x + 1, (0, ny + 1)[side]] = zero_col

    load.wait()

    def relay(x):
        for y in range(ny):
            col = raw[pl.ds(x * ny + y, spec, stride=rows), :]
            ext[x + 1, y + 1] = jnp.concatenate([col, jnp.zeros((pad - spec, nz), F32)], axis=0)

    relay(0)
    relay(nx - 1)
    neighbours = sum(has.astype(jnp.int32) for has in has_x + has_y)
    pl.semaphore_wait(barrier, neighbours)
    for c in range(chunks):
        for side in (0, 1):
            @pl.when(has_x[side])
            def _():
                x_copy(0, side, c).start()
    for x in range(1, nx - 1):
        relay(x)
    for side in (0, 1):
        @pl.when(has_y[side])
        def _():
            y_copy(0, side).start()

    square[...] = jnp.zeros_like(square)

    def split_weight(value):
        square[0:spec, 0:spec] = value
        w = square[...]
        high = w.astype(BF16).astype(F32)
        both = (high + pltpu.roll(w - high, 64, 1)).astype(BF16)
        return jnp.concatenate([both, both], axis=1)

    mix_w[...] = split_weight(mixing_ref[...])
    for k in range(nclass):
        inv_w[k * 64:(k + 1) * 64, :] = split_weight(inverses_ref[k])
    square[...] = jnp.zeros_like(square)
    square[0:1, 0:spec] = diffusion_ref[...]
    line = jnp.broadcast_to(square[0:1, :], square.shape)
    on = lax.broadcasted_iota(jnp.int32, square.shape, 0) == lax.broadcasted_iota(
        jnp.int32, square.shape, 1)
    column = jnp.sum(jnp.where(on, line, 0.0), axis=1, keepdims=True)
    coef[...] = jnp.broadcast_to(column[:pad], coef.shape)

    lane = lax.broadcasted_iota(jnp.int32, (pad, nz), 1)

    def laplace(buf, x, y):
        v = buf[x + 1, y + 1]
        total = buf[x + 2, y + 1] + buf[x, y + 1] + buf[x + 1, y + 2] + buf[x + 1, y]
        total = total + jnp.where(lane == nz - 1, 0.0, pltpu.roll(v, nz - 1, 1))
        total = total + jnp.where(lane == 0, 0.0, pltpu.roll(v, 1, 1))
        return v, total - 6.0 * v

    def split_rows(v):
        v = jnp.concatenate([v, jnp.zeros((64 - pad, v.shape[1]), F32)], axis=0)
        high = v.astype(BF16)
        low = (v - high.astype(F32)).astype(BF16)
        return jnp.concatenate([high, high, low, low], axis=0)

    def solve(xs, c):
        cells = [(x, c * CHUNK + j) for x in xs for j in range(CHUNK)]
        parts = []
        for x, y in cells:
            v, lap = laplace(ext, x, y)
            force = coef[...] * lap
            forcing[x, y] = force
            parts.append(v + force)
        start = jnp.concatenate(parts, axis=1)
        target[...] = start
        which = jnp.concatenate([class_ref[pl.ds(x * ny + y, 1), :] for x, y in cells], axis=1)
        cell_rate = jnp.zeros(which.shape, F32)
        cell_count = jnp.zeros(which.shape, jnp.int32)
        for k in range(nclass):
            cell_rate = jnp.where(which == k, rate_ref[k], cell_rate)
            cell_count = jnp.where(which == k, counts_ref[k], cell_count)

        def step(k, y):
            product = jnp.dot(mix_w[...], split_rows(jnp.tanh(y)), preferred_element_type=F32)[:pad]
            residual = y - target[...] - cell_rate * (product - y)
            fixes = jnp.dot(inv_w[...], split_rows(residual), preferred_element_type=F32)
            active = jnp.where(k < cell_count, which, nclass)
            fix = jnp.zeros_like(y)
            for n in range(nclass):
                fix = jnp.where(active == n, fixes[n * 64:n * 64 + pad], fix)
            return y - fix

        value = lax.fori_loop(0, NMAX, step, start)
        for i, (x, y) in enumerate(cells):
            ext2[x + 1, y + 1] = value[:, i * nz:(i + 1) * nz]

    y_arrive(0)

    def inner(c, carry):
        solve(tuple(range(1, nx - 1)), c)
        return carry

    def outer(c, carry):
        x_arrive(0, c)
        solve((0, nx - 1), c)
        for side in (0, 1):
            @pl.when(has_x[side])
            def _():
                x_copy(1, side, c).start()
        return carry

    if nx > 2:
        lax.fori_loop(0, chunks, inner, 0)
    lax.fori_loop(0, chunks, outer, 0)
    for side in (0, 1):
        @pl.when(has_y[side])
        def _():
            y_copy(1, side).start()

    def finish(x, y):
        v, lap = laplace(ext2, x, y)
        new = v + 0.5 * (coef[...] * lap - forcing[x, y])
        out_ref[pl.ds(x * ny + y, spec, stride=rows), :] = new[:spec]

    for x in range(1, nx - 1):
        for y in range(1, ny - 1):
            finish(x, y)
    y_arrive(1)
    for x in range(1, nx - 1):
        finish(x, 0)
        finish(x, ny - 1)

    def last(c, carry):
        x_arrive(1, c)
        for j in range(CHUNK):
            for x in (0, nx - 1):
                finish(x, c * CHUNK + j)
        return carry

    lax.fori_loop(0, chunks, last, 0)

    for stage in (0, 1):
        for side in (0, 1):
            @pl.when(has_x[side])
            def _():
                for c in range(chunks):
                    x_copy(stage, side, c).wait_send()
            @pl.when(has_y[side])
            def _():
                y_copy(stage, side).wait_send()


def local(species, diffusion, class_rate, mixing, inverses, newton_counts, cell_class):
    spec, nx, ny, nz = species.shape
    nclass = inverses.shape[0]
    pad = -(-spec // 8) * 8
    chunks = ny // CHUNK
    width = 2 * CHUNK * nz
    vmem = pl.BlockSpec(memory_space=pltpu.VMEM)
    smem = pl.BlockSpec(memory_space=pltpu.SMEM)
    out = pl.pallas_call(
        functools.partial(kernel, (spec, nx, ny, nz, nclass)),
        out_shape=jax.ShapeDtypeStruct((spec * nx * ny, nz), F32),
        in_specs=[pl.BlockSpec(memory_space=pl.ANY), vmem, smem, vmem, vmem, smem, vmem],
        out_specs=vmem,
        scratch_shapes=[
            pltpu.VMEM((spec * nx * ny, nz), F32),
            pltpu.VMEM((nx + 2, ny + 2, pad, nz), F32),
            pltpu.VMEM((nx + 2, ny + 2, pad, nz), F32),
            pltpu.VMEM((nx, ny, pad, nz), F32),
            pltpu.VMEM((pad, width), F32),
            pltpu.VMEM((pad, nz), F32),
            pltpu.VMEM((64, 128), F32),
            pltpu.VMEM((64, 256), BF16),
            pltpu.VMEM((nclass * 64, 256), BF16),
            pltpu.SemaphoreType.DMA(()),
            pltpu.SemaphoreType.DMA((2, 2, chunks)),
            pltpu.SemaphoreType.DMA((2, 2, chunks)),
            pltpu.SemaphoreType.DMA((2, 2)),
            pltpu.SemaphoreType.DMA((2, 2)),
        ],
        compiler_params=pltpu.CompilerParams(
            collective_id=0, has_side_effects=True, vmem_limit_bytes=40 * 1024 * 1024),
    )(
        species.reshape(spec * nx * ny, nz), diffusion.reshape(1, spec), class_rate,
        mixing, inverses, newton_counts, cell_class.reshape(nx * ny, nz),
    )
    return out.reshape(species.shape)


def solution(mesh):
    in_specs = (P(None, "gx", "gy", None), P(), P(), P(), P(), P(), P("gx", "gy", None))
    out_specs = P(None, "gx", "gy", None)
    return jax.shard_map(local, mesh=mesh, in_specs=in_specs, out_specs=out_specs, check_vma=False)
```

time: 225 us -> 42.6 us (0.19)
  the two profiles are of different devices: /device:TPU:20 before, /device:TPU:1 now
where the time goes in v1:
time: 42.6 us; the launch traced here: 42.5 us
  Pallas kernels  39.3 us (92%)
  local copies, waits for them, and re-layouts  3.04 us (7%)
    pallas_call x1, Pallas kernels, local(): pl.pallas_call(functools.partial(kernel, (spec, nx, ny, nz, nclass)), out...  39.3 us
    unnamed x14, local copies, waits for them, and re-layouts  3.04 us

profile of v1, /device:TPU:1, one launch (start us, length us, event | category | flops | bytes accessed | tf_op | source)
XLA Modules:
  0.0 42.5 jit_solution(7494209619411257039)
XLA Ops:
  0.0 0.0 copy-start.1
  0.0 0.0 copy-start.2
  0.0 0.0 copy-start.3
  0.0 0.0 copy-start.4
  0.0 0.0 copy-start.5
  0.0 1.0 %copy.8.inverses_ref = f32[4,53,53]{2,1,0:T(8,128)S(1)} copy(f32[4,53,53]{2,0,1:T(4,128)} %param.11) | data formatting | bytes 89888 | tf_op args[4]
  1.0 0.0 copy-done.1
  1.0 0.0 copy-done.2
  1.0 0.0 copy-done.3
  1.0 0.0 copy-done.4
  1.0 0.0 copy-done.5
  1.0 0.0 copy-start
  1.0 1.2 %copy-done = f32[53,4,8,128]{3,2,1,0:T(8,128)S(1)} copy-done((f32[53,4,8,128]{3,2,1,0:T(8,128)S(1)}, f32[53,4,8,128]{3,2,1,0:T(8,128)}, u32[]{:S(2)}) %copy-start) | copy-done | bytes 868376
  2.2 39.3 %shard_map.73 = f32[1696,128]{1,0:T(8,128)S(1)} custom-call(f32[1696,128]{1,0:T(8,128)S(1)} %bitcast.5, f32[1,53]{1,0:T(1,128)S(1)} %bitcast.7, f32[4]{0:T(128)S(1)} %copy-done.4, f32[53,53]{1,0:T(8,128)S(1)} %copy-done.1, f32[4,53,53]{2,1,0:T(8,128)S(1)} %copy.8.inverses_ref, s32[4]{0:T(128)S(1)} %copy-done.5, s32[32,128]{1,0:T(8,128)S(1)} %bitcast.6), custom_call_target="tpu_custom_call" | custom-call | tf_op jit(solution)/shard_map/pallas_call | solution.py:239
  41.5 0.9 %copy.10 = f32[53,4,8,128]{3,2,1,0:T(8,128)} copy(f32[53,4,8,128]{3,2,1,0:T(8,128)S(1)} %bitcast.4) | data formatting | bytes 1736704
Async XLA Ops:
  0.0 1.0 %copy-start.1 = (f32[53,53]{1,0:T(8,128)S(1)}, f32[53,53]{1,0:T(8,128)}, u32[]{:S(2)}) copy-start(f32[53,53]{1,0:T(8,128)} %mixing_ref.1) | copy-start | bytes 33712
  0.0 1.0 %copy-start.2 = (s32[4,8,128]{2,1,0:T(8,128)S(1)}, s32[4,8,128]{2,1,0:T(8,128)}, u32[]{:S(2)}) copy-start(s32[4,8,128]{2,1,0:T(8,128)} %param.13) | copy-start | bytes 49156
  0.0 1.0 %copy-start.3 = (f32[53]{0:T(128)S(1)}, f32[53]{0:T(128)}, u32[]{:S(2)}) copy-start(f32[53]{0:T(128)} %param.8) | copy-start | bytes 640
  0.0 1.0 %copy-start.4 = (f32[4]{0:T(128)S(1)}, f32[4]{0:T(128)}, u32[]{:S(2)}) copy-start(f32[4]{0:T(128)} %rate_ref.1) | copy-start | bytes 52
  0.0 1.0 %copy-start.5 = (s32[4]{0:T(128)S(1)}, s32[4]{0:T(128)}, u32[]{:S(2)}) copy-start(s32[4]{0:T(128)} %counts_ref.1) | copy-start | bytes 52
  1.0 1.2 %copy-start = (f32[53,4,8,128]{3,2,1,0:T(8,128)S(1)}, f32[53,4,8,128]{3,2,1,0:T(8,128)}, u32[]{:S(2)}) copy-start(f32[53,4,8,128]{3,2,1,0:T(8,128)} %param.7) | copy-start | bytes 2605060

commit v2 on v1

--- a/solution.py
+++ b/solution.py
@@ -9,6 +9,9 @@
 
 NMAX = 8
 CHUNK = 2
+GROUP = 1
+SPAN = 4
+UNROLL = 4
 MESH = pl.DeviceIdType.MESH
 F32 = jnp.float32
 BF16 = jnp.bfloat16
@@ -35,6 +38,15 @@
     load = pltpu.make_async_copy(species_hbm, raw, load_sem)
     load.start()
 
+    zero_col = jnp.zeros((pad, nz), F32)
+    for buf in (ext, ext2):
+        for y in range(ny):
+            buf[0, y + 1] = zero_col
+            buf[nx + 1, y + 1] = zero_col
+        for x in range(nx):
+            buf[x + 1, 0] = zero_col
+            buf[x + 1, ny + 1] = zero_col
+
     barrier = pltpu.get_barrier_semaphore()
     for has, to in zip(has_x + has_y, to_x + to_y):
         @pl.when(has)
@@ -46,7 +58,7 @@
         src_row, dst_row = (1, nx + 1) if side == 0 else (nx, 0)
         ys = pl.ds(1 + c * CHUNK, CHUNK)
         return pltpu.make_async_remote_copy(
-            src_ref=buf.at[src_row, ys], dst_ref=buf.at[dst_row, ys],
+            src_ref=buf.at[src_row, ys, pl.ds(0, spec)], dst_ref=buf.at[dst_row, ys, pl.ds(0, spec)],
             send_sem=xs_send.at[stage, side, c], recv_sem=xs_recv.at[stage, side, c],
             device_id=to_x[side], device_id_type=MESH)
 
@@ -54,7 +66,8 @@
         buf = (ext, ext2)[stage]
         src_col, dst_col = (1, ny + 1) if side == 0 else (ny, 0)
         return pltpu.make_async_remote_copy(
-            src_ref=buf.at[pl.ds(1, nx), src_col], dst_ref=buf.at[pl.ds(1, nx), dst_col],
+            src_ref=buf.at[pl.ds(1, nx), src_col, pl.ds(0, spec)],
+            dst_ref=buf.at[pl.ds(1, nx), dst_col, pl.ds(0, spec)],
             send_sem=ys_send.at[stage, side], recv_sem=ys_recv.at[stage, side],
             device_id=to_y[side], device_id_type=MESH)
 
@@ -69,19 +82,6 @@
             @pl.when(has_y[side])
             def _():
                 y_copy(stage, 1 - side).wait_recv()
-
-    zero_col = jnp.zeros((pad, nz), F32)
-    for side in (0, 1):
-        @pl.when(jnp.logical_not(has_x[side]))
-        def _():
-            for buf in (ext, ext2):
-                for y in range(ny):
-                    buf[(0, nx + 1)[side], y + 1] = zero_col
-        @pl.when(jnp.logical_not(has_y[side]))
-        def _():
-            for buf in (ext, ext2):
-                for x in range(nx):
-                    buf[x + 1, (0, ny + 1)[side]] = zero_col
 
     load.wait()
 
@@ -112,12 +112,12 @@
         square[0:spec, 0:spec] = value
         w = square[...]
         high = w.astype(BF16).astype(F32)
-        both = (high + pltpu.roll(w - high, 64, 1)).astype(BF16)
-        return jnp.concatenate([both, both], axis=1)
-
-    mix_w[...] = split_weight(mixing_ref[...])
-    for k in range(nclass):
-        inv_w[k * 64:(k + 1) * 64, :] = split_weight(inverses_ref[k])
+        both = high + pltpu.roll((w - high).astype(BF16).astype(F32), 64, 1)
+        return jnp.concatenate([both, both], axis=1)[:, :192]
+
+    mix_w[...] = split_weight(mixing_ref[...]).astype(BF16)
+    inv_w[...] = jnp.concatenate(
+        [split_weight(inverses_ref[:, k, :])[:pad] for k in range(nclass)], axis=0).astype(BF16)
     square[...] = jnp.zeros_like(square)
     square[0:1, 0:spec] = diffusion_ref[...]
     line = jnp.broadcast_to(square[0:1, :], square.shape)
@@ -139,57 +139,75 @@
         v = jnp.concatenate([v, jnp.zeros((64 - pad, v.shape[1]), F32)], axis=0)
         high = v.astype(BF16)
         low = (v - high.astype(F32)).astype(BF16)
-        return jnp.concatenate([high, high, low, low], axis=0)
-
-    def solve(xs, c):
-        cells = [(x, c * CHUNK + j) for x in xs for j in range(CHUNK)]
-        parts = []
-        for x, y in cells:
-            v, lap = laplace(ext, x, y)
-            force = coef[...] * lap
-            forcing[x, y] = force
-            parts.append(v + force)
-        start = jnp.concatenate(parts, axis=1)
-        target[...] = start
-        which = jnp.concatenate([class_ref[pl.ds(x * ny + y, 1), :] for x, y in cells], axis=1)
-        cell_rate = jnp.zeros(which.shape, F32)
-        cell_count = jnp.zeros(which.shape, jnp.int32)
-        for k in range(nclass):
-            cell_rate = jnp.where(which == k, rate_ref[k], cell_rate)
-            cell_count = jnp.where(which == k, counts_ref[k], cell_count)
-
-        def step(k, y):
-            product = jnp.dot(mix_w[...], split_rows(jnp.tanh(y)), preferred_element_type=F32)[:pad]
-            residual = y - target[...] - cell_rate * (product - y)
-            fixes = jnp.dot(inv_w[...], split_rows(residual), preferred_element_type=F32)
-            active = jnp.where(k < cell_count, which, nclass)
-            fix = jnp.zeros_like(y)
-            for n in range(nclass):
-                fix = jnp.where(active == n, fixes[n * 64:n * 64 + pad], fix)
-            return y - fix
-
-        value = lax.fori_loop(0, NMAX, step, start)
-        for i, (x, y) in enumerate(cells):
-            ext2[x + 1, y + 1] = value[:, i * nz:(i + 1) * nz]
+        return jnp.concatenate([high, high, low], axis=0)
+
+    def solve(xs, first):
+        groups = [[(x, first + g * GROUP + j) for x in xs for j in range(GROUP)]
+                  for g in range(SPAN // GROUP)]
+        starts, rates, whiches, limits = [], [], [], []
+        for g, cells in enumerate(groups):
+            parts = []
+            for x, y in cells:
+                v, lap = laplace(ext, x, y)
+                force = coef[...] * lap
+                forcing[x, y] = force
+                parts.append(v + force)
+            start = jnp.concatenate(parts, axis=1)
+            target[g] = start
+            which = jnp.concatenate([class_ref[pl.ds(x * ny + y, 1), :] for x, y in cells], axis=1)
+            cell_rate = jnp.zeros(which.shape, F32)
+            cell_count = jnp.zeros(which.shape, jnp.int32)
+            for k in range(nclass):
+                cell_rate = jnp.where(which == k, rate_ref[k], cell_rate)
+                cell_count = jnp.where(which == k, counts_ref[k], cell_count)
+            starts.append(start)
+            rates.append(cell_rate)
+            whiches.append(which)
+            limits.append(cell_count)
+
+        def step(k, ys):
+            out = []
+            for g, y in enumerate(ys):
+                product = jnp.dot(mix_w[...], split_rows(jnp.tanh(y)), preferred_element_type=F32)[:pad]
+                residual = y - target[g] - rates[g] * (product - y)
+                fixes = jnp.dot(inv_w[...], split_rows(residual), preferred_element_type=F32)
+                active = jnp.where(k < limits[g], whiches[g], nclass)
+                fix = jnp.zeros_like(y)
+                for n in range(nclass):
+                    fix = jnp.where(active == n, fixes[n * pad:(n + 1) * pad], fix)
+                out.append(y - fix)
+            return tuple(out)
+
+        values = lax.fori_loop(0, NMAX, step, tuple(starts), unroll=UNROLL)
+        for cells, value in zip(groups, values):
+            for i, (x, y) in enumerate(cells):
+                ext2[x + 1, y + 1] = value[:, i * nz:(i + 1) * nz]
 
     y_arrive(0)
 
     def inner(c, carry):
-        solve(tuple(range(1, nx - 1)), c)
+        solve(tuple(range(1, nx - 1)), c * SPAN)
         return carry
 
     def outer(c, carry):
-        x_arrive(0, c)
-        solve((0, nx - 1), c)
-        for side in (0, 1):
-            @pl.when(has_x[side])
-            def _():
-                x_copy(1, side, c).start()
+        per = SPAN // CHUNK
+        for i in range(per):
+            x_arrive(0, c * per + i)
+        solve((0, nx - 1), c * SPAN)
+        for side in (0, 1):
+            @pl.when(has_x[side])
+            def _():
+                for i in range(per):
+                    x_copy(1, side, c * per + i).start()
         return carry
 
+    spans = ny // SPAN
+    early = (spans + 1) // 2
     if nx > 2:
-        lax.fori_loop(0, chunks, inner, 0)
-    lax.fori_loop(0, chunks, outer, 0)
+        lax.fori_loop(0, early, inner, 0)
+    lax.fori_loop(0, spans, outer, 0)
+    if nx > 2:
+        lax.fori_loop(early, spans, inner, 0)
     for side in (0, 1):
         @pl.when(has_y[side])
         def _():
@@ -233,7 +251,7 @@
     nclass = inverses.shape[0]
     pad = -(-spec // 8) * 8
     chunks = ny // CHUNK
-    width = 2 * CHUNK * nz
+    width = 2 * GROUP * nz
     vmem = pl.BlockSpec(memory_space=pltpu.VMEM)
     smem = pl.BlockSpec(memory_space=pltpu.SMEM)
     out = pl.pallas_call(
@@ -246,11 +264,11 @@
             pltpu.VMEM((nx + 2, ny + 2, pad, nz), F32),
             pltpu.VMEM((nx + 2, ny + 2, pad, nz), F32),
             pltpu.VMEM((nx, ny, pad, nz), F32),
-            pltpu.VMEM((pad, width), F32),
+            pltpu.VMEM((SPAN // GROUP, pad, width), F32),
             pltpu.VMEM((pad, nz), F32),
             pltpu.VMEM((64, 128), F32),
-            pltpu.VMEM((64, 256), BF16),
-            pltpu.VMEM((nclass * 64, 256), BF16),
+            pltpu.VMEM((64, 192), BF16),
+            pltpu.VMEM((nclass * pad, 192), BF16),
             pltpu.SemaphoreType.DMA(()),
             pltpu.SemaphoreType.DMA((2, 2, chunks)),
             pltpu.SemaphoreType.DMA((2, 2, chunks)),
@@ -258,10 +276,10 @@
             pltpu.SemaphoreType.DMA((2, 2)),
         ],
         compiler_params=pltpu.CompilerParams(
-            collective_id=0, has_side_effects=True, vmem_limit_bytes=40 * 1024 * 1024),
+            collective_id=0, has_side_effects=True, vmem_limit_bytes=60 * 1024 * 1024),
     )(
         species.reshape(spec * nx * ny, nz), diffusion.reshape(1, spec), class_rate,
-        mixing, inverses, newton_counts, cell_class.reshape(nx * ny, nz),
+        mixing, inverses.transpose(1, 0, 2), newton_counts, cell_class.reshape(nx * ny, nz),
     )
     return out.reshape(species.shape)
 

time: 42.6 us -> 33.2 us (0.78)
  the two profiles are of different devices: /device:TPU:1 before, /device:TPU:19 now
where the time goes in v2:
time: 33.2 us; the launch traced here: 33 us
  Pallas kernels  30.9 us (93%)
  local copies, waits for them, and re-layouts  2.12 us (6%)
    pallas_call x1, Pallas kernels, local(): pl.pallas_call(functools.partial(kernel, (spec, nx, ny, nz, nclass)), out...  30.9 us
    unnamed x1, local copies, waits for them, and re-layouts  2.12 us

profile of v2, /device:TPU:19, one launch (start us, length us, event | category | flops | bytes accessed | tf_op | source)
XLA Modules:
  0.0 33.0 jit_solution(1585693026186209160)
XLA Ops:
  0.0 30.9 %shard_map.73 = f32[1696,128]{1,0:T(8,128)} custom-call(f32[1696,128]{1,0:T(8,128)} %bitcast.6, f32[1,53]{1,0:T(1,128)} %bitcast.9, f32[4]{0:T(128)} %rate_ref.1, f32[53,53]{1,0:T(8,128)} %mixing_ref.1, f32[53,4,53]{2,1,0:T(4,128)} %bitcast.7, s32[4]{0:T(128)} %counts_ref.1, s32[32,128]{1,0:T(8,128)} %bitcast.8), custom_call_target="tpu_custom_call" | custom-call | tf_op jit(solution)/shard_map/pallas_call | solution.py:257
  30.9 2.1 %copy.9 = f32[53,4,8,128]{3,2,1,0:T(8,128)} copy(f32[53,4,8,128]{3,2,1,0:T(8,128)} %bitcast.5) | data formatting | bytes 1736704

commit v3 on v2

--- a/solution.py
+++ b/solution.py
@@ -11,7 +11,7 @@
 CHUNK = 2
 GROUP = 1
 SPAN = 4
-UNROLL = 4
+UNROLL = 8
 MESH = pl.DeviceIdType.MESH
 F32 = jnp.float32
 BF16 = jnp.bfloat16
@@ -256,7 +256,7 @@
     smem = pl.BlockSpec(memory_space=pltpu.SMEM)
     out = pl.pallas_call(
         functools.partial(kernel, (spec, nx, ny, nz, nclass)),
-        out_shape=jax.ShapeDtypeStruct((spec * nx * ny, nz), F32),
+        out_shape=pltpu.VMEM((spec * nx * ny, nz), F32),
         in_specs=[pl.BlockSpec(memory_space=pl.ANY), vmem, smem, vmem, vmem, smem, vmem],
         out_specs=vmem,
         scratch_shapes=[

time: 33.2 us -> 30.3 us (0.913)
  Pallas kernels: 30.9 us -> 29.2 us
  local copies, waits for them, and re-layouts: 2.12 us -> 0.91 us
    pallas_call x1, Pallas kernels: 30.9 us -> 29.2 us  [local(): pl.pallas_call(functools.partial(kernel, (spec, nx, ny, nz, nclass)), out...]
    unnamed x1, local copies, waits for them, and re-layouts: 2.12 us -> 0.91 us
where the time goes in v3:
time: 30.3 us; the launch traced here: 30.1 us
  Pallas kernels  29.2 us (96%)
  local copies, waits for them, and re-layouts  0.91 us (3%)
    pallas_call x1, Pallas kernels, local(): pl.pallas_call(functools.partial(kernel, (spec, nx, ny, nz, nclass)), out...  29.2 us
    unnamed x1, local copies, waits for them, and re-layouts  0.91 us

profile of v3, /device:TPU:19, one launch (start us, length us, event | category | flops | bytes accessed | tf_op | source)
XLA Modules:
  0.0 30.1 jit_solution(7063981935735111660)
XLA Ops:
  0.0 29.2 %shard_map.73 = f32[1696,128]{1,0:T(8,128)S(1)} custom-call(f32[1696,128]{1,0:T(8,128)} %bitcast.6, f32[1,53]{1,0:T(1,128)} %bitcast.9, f32[4]{0:T(128)} %rate_ref.1, f32[53,53]{1,0:T(8,128)} %mixing_ref.1, f32[53,4,53]{2,1,0:T(4,128)} %bitcast.7, s32[4]{0:T(128)} %counts_ref.1, s32[32,128]{1,0:T(8,128)} %bitcast.8), custom_call_target="tpu_custom_call" | custom-call | tf_op jit(solution)/shard_map/pallas_call | solution.py:257
  29.2 0.9 %copy.9 = f32[53,4,8,128]{3,2,1,0:T(8,128)} copy(f32[53,4,8,128]{3,2,1,0:T(8,128)S(1)} %bitcast.5) | data formatting | bytes 1736704
